TPU v7x, 256 devices: a whole 4x4x8 slice. The times are simulated.
256 devices in a mesh: group: 32 (over z, y_hi, core), mp: 8 (over x, y_lo).
Axes of the slice: x: 4, y: 4 (y_hi: 2, y_lo: 2; y = y_hi * 2 + y_lo), z: 8, core: 2. Of those that a mesh axis runs over, the one named last changes fastest.
Arguments:
- anchor: float32 [16, 2048, 2048], P(None, 'group', 'mp'), may hold values from -6 to 6
- momentum: float32 [16, 2048, 2048], P(None, 'group', 'mp'), may hold values from -3 to 3
- deltas: float32 [32, 2, 2048, 2048], P('group', None, None, 'mp'), may hold values from -3 to 3
- old_path: int32 [32, 2], replicated, may hold values from 0 to 7, as said below
- new_path: int32 [32, 2], replicated, may hold values from 0 to 7, as said below
- tokens: bfloat16 [32, 1024, 2048], P('group', None, 'mp'), may hold values from -40 to 40
- cotangent: bfloat16 [32, 1024, 2048], P('group', None, 'mp'), may hold values from -6 to 6
Outputs:
- new_anchor: float32 [16, 2048, 2048], P(None, 'group', 'mp')
- new_momentum: float32 [16, 2048, 2048], P(None, 'group', 'mp')
- grads: bfloat16 [32, 2, 2048, 2048], P('group', None, None, 'mp')
Inputs may be any that keep to these rules, and one draw needn't show every extreme that they name: `old_path`: for each of the 2 levels, every one of the 8 modules is named by at least one group. `new_path`: for each of the 2 levels, every one of the 8 modules is named by at least one group.
All inputs are finite; a program needn't handle non-finite values.
Results may differ from a plain program's by a relative error of at most 0.014.
Values may be sent and summed in bfloat16 or wider, within the bound.
A program may use at most 128 MiB of HBM per device.

v0:
```python
import math

import jax
import jax.numpy as jnp
from jax import lax
from jax.sharding import Mesh
from jax.sharding import PartitionSpec as P

D = 2048
MODS = 8
MP = ("mp_0", "mp_1")


outer_rate = 0.7
momentum_rate = 0.9
epsilon = 1e-06


def whole_of(x, axes, dim):
    for axis in reversed(axes):
        x = lax.all_gather(x, axis, axis=dim, tiled=True)
    return x


def cut_along(x, dim, length):
    before, after = (x.shape[:dim], x.shape[dim + 1 :])
    return jnp.moveaxis(x.reshape(*before, length, -1, *after), dim, 0)


def summed_on_arrival(x, axis, dim):
    length = lax.axis_size(axis)
    pieces = lax.all_to_all(cut_along(x, dim, length), axis, 0, 0, tiled=True)
    return jnp.sum(pieces.astype(jnp.float32), axis=0)


def silu_slope(values):
    sigmoid_part = jax.nn.sigmoid(values)
    return sigmoid_part * (1.0 + values * (1.0 - sigmoid_part))


def normalize(hidden):
    whole = whole_of(hidden, MP, 1)
    values = whole.astype(jnp.float32)
    scale = lax.rsqrt(jnp.mean(values * values, axis=-1) + epsilon)
    normed = (values * scale[:, None]).astype(jnp.bfloat16)
    return (normed, scale)


def outer_update(received, anchor_rows, momentum_rows, old_columns, new_columns):
    groups_count = received.shape[0]
    levels_count = received.shape[1]
    module_count = anchor_rows.shape[0]
    offsets = jnp.arange(levels_count, dtype=jnp.int32) * MODS
    old_index = (old_columns + offsets[None, :]).reshape(-1)
    selector = (old_index[None, :] == jnp.arange(module_count, dtype=jnp.int32)[:, None]).astype(
        jnp.float32
    )
    sums = jnp.dot(
        selector, received.reshape(groups_count * levels_count, -1), precision=lax.Precision.HIGHEST
    )
    counts = jnp.sum(selector, axis=1)
    outer_grad = (sums / counts[:, None]).reshape(anchor_rows.shape)
    new_momentum = momentum_rate * momentum_rows + outer_grad
    new_anchor = anchor_rows - outer_rate * (outer_grad + momentum_rate * new_momentum)
    new_index = new_columns + offsets[None, :]
    outgoing = jnp.take(new_anchor, new_index, axis=0).astype(jnp.bfloat16)
    return (new_anchor, new_momentum, outgoing)


def shards(anchor, momentum, deltas, old_path, new_path, tokens, cotangent):
    factor = 1.0 / math.sqrt(D)
    first_state = tokens[0]
    upstream = cotangent[0].astype(jnp.float32)
    first_normed, first_scale = normalize(first_state)
    received = lax.all_to_all(
        deltas.astype(jnp.bfloat16), "group", split_axis=2, concat_axis=0, tiled=True
    ).astype(deltas.dtype)
    new_anchor, new_momentum, outgoing = outer_update(
        received, anchor, momentum, old_path, new_path
    )
    loaded = lax.all_to_all(outgoing, "group", split_axis=0, concat_axis=2, tiled=True)
    weight_parts = [loaded[0, 0], loaded[0, 1]]
    first_weight = weight_parts[0]
    second_weight = weight_parts[1]
    first_pre = jnp.dot(first_normed, first_weight, preferred_element_type=jnp.float32) * factor
    second_state = (first_state.astype(jnp.float32) + jax.nn.silu(first_pre)).astype(jnp.bfloat16)
    second_normed, second_scale = normalize(second_state)
    second_pre = jnp.dot(second_normed, second_weight, preferred_element_type=jnp.float32) * factor
    second_slope = (upstream * silu_slope(second_pre)).astype(jnp.bfloat16)
    second_grad = (
        lax.dot_general(
            second_normed,
            second_slope,
            (((0,), (0,)), ((), ())),
            preferred_element_type=jnp.float32,
        )
        * factor
    ).astype(jnp.bfloat16)
    terms = (
        lax.dot_general(
            second_slope,
            second_weight,
            (((1,), (1,)), ((), ())),
            preferred_element_type=jnp.float32,
        )
        * factor
    )
    normed_grad = summed_on_arrival(terms.astype(jnp.bfloat16), MP, 1)
    middle = second_state.astype(jnp.float32)
    inner = lax.psum(jnp.sum(normed_grad * middle, axis=-1), MP)
    state_grad = (
        upstream
        + second_scale[:, None] * normed_grad
        - middle * (second_scale**3 * inner / D)[:, None]
    )
    first_slope = (state_grad * silu_slope(first_pre)).astype(jnp.bfloat16)
    first_grad = (
        lax.dot_general(
            first_normed, first_slope, (((0,), (0,)), ((), ())), preferred_element_type=jnp.float32
        )
        * factor
    ).astype(jnp.bfloat16)
    grads = jnp.stack([first_grad, second_grad])[None]
    return (new_anchor, new_momentum, grads)


def solution(mesh):
    split = Mesh(mesh.devices.reshape(mesh.shape["group"], 4, 2), ("group", "mp_0", "mp_1"))
    placed = (
        P(None, "group", MP),
        P(None, "group", MP),
        P("group", None, None, MP),
        P(),
        P(),
        P("group", None, MP),
        P("group", None, MP),
    )
    return jax.shard_map(
        shards,
        mesh=split,
        in_specs=placed,
        out_specs=(P(None, "group", MP), P(None, "group", MP), P("group", None, None, MP)),
        check_vma=False,
    )
```

profile of v0, /device:TPU:1, one launch (start us, length us, event | category | flops | bytes accessed | tf_op | source)
XLA Modules:
  0.0 328.3 jit_solution(7924139874974365925)
XLA Ops:
  7.2 8.6 %copy.63 = bf16[1,2,2048,256]{3,1,0,2:T(2,128)(2,1)} copy(f32[1,2,2048,256]{3,2,1,0:T(8,128)} %param.9) | data formatting | bytes 6291456 | tf_op args[2]
  15.7 12.9 %all-to-all-start = ((bf16[1,2,2048,256]{3,1,0,2:T(2,128)(2,1)}), bf16[1,2,2048,256]{3,1,0,2:T(2,128)(2,1)S(1)}, u32[]{:S(2)}, u32[]{:S(2)}) async-start(bf16[1,2,2048,256]{3,1,0,2:T(2,128)(2,1)} %copy.63), calls=%async_computation | async-start | bytes 4194304 | tf_op jit(solution)/shard_map/all_to_all | solution.py:75
  28.7 0.7 all-gather.11.cloned.1.call-update
  29.4 38.9 %all-gather.11.cloned.1.call-done = bf16[1,1024,512]{2,1,0:T(8,128)(2,1)} async-done(((bf16[1,1024,256]{2,1,0:T(8,128)(2,1)}), bf16[1,1024,512]{2,1,0:T(8,128)(2,1)}) %all-gather.11.cloned.1.call-update) | async-done | bytes 1048592 | tf_op jit(solution)/shard_map/all_gather | solution.py:21
  68.3 0.1 compare_and_fusion
  68.4 0.1 copy.48
  68.5 0.1 broadcast_add_fusion
  68.6 0.1 copy.43
  68.7 0.1 eq.15
  68.8 0.1 copy.49
  68.8 0.1 reshape.46
  69.0 0.1 convert_reduce_fusion.1
  69.1 9.6 %all-to-all-done = bf16[1,2,2048,256]{3,1,0,2:T(2,128)(2,1)S(1)} async-done(((bf16[1,2,2048,256]{3,1,0,2:T(2,128)(2,1)}), bf16[1,2,2048,256]{3,1,0,2:T(2,128)(2,1)S(1)}, u32[]{:S(2)}, u32[]{:S(2)}) %all-to-all-start) | async-done | bytes 2097184 | tf_op jit(solution)/shard_map/all_to_all | solution.py:75
  78.7 0.4 copy.45
  79.1 1.3 copy.59
  80.4 0.4 convolution_divide_fusion
  80.8 0.3 copy.60
  81.1 0.5 copy-done.7
  81.7 0.4 copy-done.8
  82.1 1.3 fusion.34
  83.4 0.8 gather_fusion
  84.2 1.7 select_convert_fusion
  85.9 6.5 %all-to-all-start.1 = ((bf16[32,2,64,256]{3,2,1,0:T(8,128)(2,1)}), bf16[32,2,64,256]{3,2,1,0:T(8,128)(2,1)S(1)}, u32[]{:S(2)}, u32[]{:S(2)}) async-start(bf16[32,2,64,256]{3,2,1,0:T(8,128)(2,1)} %select_convert_fusion), calls=%async_computation.1 | async-start | bytes 4194304 | tf_op jit(solution)/shard_map/all_to_all | solution.py:81
  92.5 0.2 copy.47
  92.7 28.1 %all-gather.13.cloned.1.call-done = bf16[1,1024,2048]{2,1,0:T(8,128)(2,1)} async-done(((bf16[1,1024,512]{2,1,0:T(8,128)(2,1)}), bf16[1,1024,2048]{2,1,0:T(8,128)(2,1)}) %all-gather.13.cloned.1.call-update) | async-done | bytes 4194320 | tf_op jit(solution)/shard_map/all_gather | solution.py:21
  120.8 3.1 fusion.2
  123.9 18.6 %all-to-all-done.1 = bf16[32,2,64,256]{3,2,1,0:T(8,128)(2,1)S(1)} async-done(((bf16[32,2,64,256]{3,2,1,0:T(8,128)(2,1)}), bf16[32,2,64,256]{3,2,1,0:T(8,128)(2,1)S(1)}, u32[]{:S(2)}, u32[]{:S(2)}) %all-to-all-start.1) | async-done | bytes 2097184 | tf_op jit(solution)/shard_map/all_to_all | solution.py:81
  142.5 0.1 copy.50
  142.6 2.8 copy-done.1
  145.4 2.8 fusion.35
  148.3 0.2 all-gather.9.cloned.1.call-start
  148.5 23.5 %all-gather.7.cloned.1.call-done = bf16[1024,512]{0,1:T(8,128)(2,1)} async-done(((bf16[1024,256]{0,1:T(8,128)(2,1)}), bf16[1024,512]{0,1:T(8,128)(2,1)}) %all-gather.7.cloned.1.call-update) | async-done | bytes 1048592 | tf_op jit(solution)/shard_map/all_gather | solution.py:21
  172.1 0.2 copy.46
  172.3 53.2 %all-gather.9.cloned.1.call-done = bf16[1024,2048]{0,1:T(8,128)(2,1)} async-done(((bf16[1024,512]{0,1:T(8,128)(2,1)}), bf16[1024,2048]{0,1:T(8,128)(2,1)}) %all-gather.9.cloned.1.call-update) | async-done | bytes 4194320 | tf_op jit(solution)/shard_map/all_gather | solution.py:21
  225.5 3.3 fusion
  228.8 0.2 copy-done.2
  228.9 1.3 fusion.25
  230.3 1.6 multiply_convert_fusion
  231.9 2.2 copy.64
  234.1 4.7 %all-to-all-start.2 = ((bf16[8,1024,256]{2,1,0:T(8,128)(2,1)}), bf16[8,1024,256]{2,1,0:T(8,128)(2,1)}, u32[]{:S(2)}, u32[]{:S(2)}) async-start(bf16[8,1024,256]{2,1,0:T(8,128)(2,1)} %bitcast.70), calls=%async_computation.2 | async-start | bytes 8388608 | tf_op jit(solution)/shard_map/all_to_all | solution.py:32
  238.9 4.6 %fusion.15 = bf16[1,2048,256]{2,1,0:T(8,128)(2,1)} fusion(bf16[1024,2048]{0,1:T(8,128)(2,1)} %all-gather.9.cloned.1.call-done, f32[1024]{0:T(1024)S(1)} %add_rsqrt_fusion, f32[1024,256]{0,1:T(8,128)S(1)} %copy-done.14, bf16[1,1024,256]{1,2,0:T(8,128)(2,1)S(1)} %copy.46), kind=kOutput, calls=%fused_computation.21 | convolution fusion | flops 1083703296 | bytes 6819840 | tf_op jit(solution)/shard_map/dot_general | solution.py:91
  243.5 54.3 %all-to-all-done.2 = bf16[8,1024,256]{2,1,0:T(8,128)(2,1)} async-done(((bf16[8,1024,256]{2,1,0:T(8,128)(2,1)}), bf16[8,1024,256]{2,1,0:T(8,128)(2,1)}, u32[]{:S(2)}, u32[]{:S(2)}) %all-to-all-start.2) | async-done | bytes 4194336 | tf_op jit(solution)/shard_map/all_to_all | solution.py:32
  297.8 2.9 convert_reduce_fusion
  300.7 0.3 copy.54
  301.0 0.2 fusion.28
  301.2 14.6 %psum.7 = f32[1024]{0:T(1024)S(1)} all-reduce(f32[1024]{0:T(1024)S(1)} %fusion.28), channel_id=1, replica_groups=mesh['group'=32,'mp_0'=4,'mp_1'=2] {'mp_0','mp_1'}, use_global_device_ids=true, to_apply=%region_5.6 | all-reduce | flops 1024 | bytes 8192 | tf_op jit(solution)/shard_map/psum | solution.py:110
  315.8 4.5 %fusion.18 = bf16[1,2048,256]{2,1,0:T(8,128)(2,1)S(1)} fusion(bf16[1,1024,2048]{2,1,0:T(8,128)(2,1)} %all-gather.13.cloned.1.call-done, f32[1024]{0:T(1024)S(1)} %add_rsqrt_fusion.1, bf16[1024,256]{0,1:T(8,128)(2,1)S(1)} %copy-done.3, f32[1024,256]{0,1:T(8,128)} %get-tuple-element.8, f32[1024,256]{0,1:T(8,128)S(1)} %copy.54, ...), kind=kOutput, calls=%fused_computation.22 | convolution fusion | flops 1085014016 | bytes 8400896 | tf_op jit(solution)/shard_map/dot_general | solution.py:118
  320.3 1.5 maximum_bitcast_fusion
  (37 shorter events, 0.3 us)
Async XLA Ops:
  15.7 52.6 %copy-start.11 = (s32[32,2]{0,1:T(2,128)S(1)}, s32[32,2]{0,1:T(2,128)}, u32[]{:S(2)}) copy-start(s32[32,2]{0,1:T(2,128)} %param.11) | copy-start | bytes 772
  15.7 52.8 %copy-start.12 = (s32[32,2]{0,1:T(2,128)S(1)}, s32[32,2]{0,1:T(2,128)}, u32[]{:S(2)}) copy-start(s32[32,2]{0,1:T(2,128)} %param.10) | copy-start | bytes 772
  15.7 62.9 %all-to-all-start = ((bf16[1,2,2048,256]{3,1,0,2:T(2,128)(2,1)}), bf16[1,2,2048,256]{3,1,0,2:T(2,128)(2,1)S(1)}, u32[]{:S(2)}, u32[]{:S(2)}) async-start(bf16[1,2,2048,256]{3,1,0,2:T(2,128)(2,1)} %copy.63), calls=%async_computation | async-start | bytes 4194304 | tf_op jit(solution)/shard_map/all_to_all | solution.py:75
  28.6 39.6 %all-gather.11.cloned.1.call-start = ((), (), s32[]{:S(2)}) async-start(), calls=%async_computation.5 | async-start | bytes 1572864 | tf_op jit(solution)/shard_map/all_gather | solution.py:21
  29.4 91.5 %all-gather.13.cloned.1.call-start = ((), (), s32[]{:S(2)}) async-start(), calls=%async_computation.6 | async-start | bytes 5242880 | tf_op jit(solution)/shard_map/all_gather | solution.py:21
  80.4 1.3 copy-start.7
  80.4 1.7 copy-start.8
  83.4 2.5 copy-start
  85.9 6.6 %copy-start.6 = (bf16[1,1024,256]{2,1,0:T(8,128)(2,1)S(1)}, bf16[1,1024,256]{2,1,0:T(8,128)(2,1)}, u32[]{:S(2)}) copy-start(bf16[1,1024,256]{2,1,0:T(8,128)(2,1)} %param.12) | copy-start | bytes 1572868
  85.9 56.6 %all-to-all-start.1 = ((bf16[32,2,64,256]{3,2,1,0:T(8,128)(2,1)}), bf16[32,2,64,256]{3,2,1,0:T(8,128)(2,1)S(1)}, u32[]{:S(2)}, u32[]{:S(2)}) async-start(bf16[32,2,64,256]{3,2,1,0:T(8,128)(2,1)} %select_convert_fusion), calls=%async_computation.1 | async-start | bytes 4194304 | tf_op jit(solution)/shard_map/all_to_all | solution.py:81
  92.4 79.6 %all-gather.7.cloned.1.call-start = ((), (), s32[]{:S(2)}) async-start(), calls=%async_computation.3 | async-start | bytes 1572864 | tf_op jit(solution)/shard_map/all_gather | solution.py:21
  142.5 2.9 copy-start.1
  142.6 5.6 %copy-start.4 = (bf16[1,2,32,64,256]{4,3,2,1,0:T(8,128)(2,1)}, bf16[1,2,32,64,256]{4,3,2,1,0:T(8,128)(2,1)S(1)}, u32[]{:S(2)}) copy-start(bf16[1,2,32,64,256]{4,3,2,1,0:T(8,128)(2,1)S(1)} %copy.50) | copy-start | bytes 6291460
  145.4 26.7 %copy-start.10 = (bf16[1,1024,256]{2,1,0:T(8,128)(2,1)S(1)}, bf16[1,1024,256]{2,1,0:T(8,128)(2,1)}, u32[]{:S(2)}) copy-start(bf16[1,1024,256]{2,1,0:T(8,128)(2,1)} %param.13) | copy-start | bytes 1572868
  148.3 80.5 %copy-start.5 = (bf16[1,2,32,64,256]{4,3,2,1,0:T(8,128)(2,1)S(1)}, bf16[1,2,32,64,256]{4,3,2,1,0:T(8,128)(2,1)}, u32[]{:S(2)}) copy-start(bf16[1,2,32,64,256]{4,3,2,1,0:T(8,128)(2,1)} %copy-done.4) | copy-start | bytes 6291460
  148.3 77.2 %all-gather.9.cloned.1.call-start = ((), (), s32[]{:S(2)}) async-start(), calls=%async_computation.4 | async-start | bytes 5242880 | tf_op jit(solution)/shard_map/all_gather | solution.py:21
  225.5 3.4 %copy-start.2 = (bf16[1024,2048]{0,1:T(8,128)(2,1)S(1)}, bf16[1024,2048]{0,1:T(8,128)(2,1)}, u32[]{:S(2)}) copy-start(bf16[1024,2048]{0,1:T(8,128)(2,1)} %all-gather.9.cloned.1.call-done) | copy-start | bytes 12582916
  230.3 1.7 copy-start.13
  234.1 4.7 %copy-start.14 = (f32[1024,256]{0,1:T(8,128)S(1)}, f32[1024,256]{0,1:T(8,128)}, u32[]{:S(2)}) copy-start(f32[1024,256]{0,1:T(8,128)} %copy-done.13) | copy-start | bytes 3145732
  234.1 63.7 %all-to-all-start.2 = ((bf16[8,1024,256]{2,1,0:T(8,128)(2,1)}), bf16[8,1024,256]{2,1,0:T(8,128)(2,1)}, u32[]{:S(2)}, u32[]{:S(2)}) async-start(bf16[8,1024,256]{2,1,0:T(8,128)(2,1)} %bitcast.70), calls=%async_computation.2 | async-start | bytes 8388608 | tf_op jit(solution)/shard_map/all_to_all | solution.py:32
  243.5 57.5 %copy-start.3 = (bf16[1024,256]{0,1:T(8,128)(2,1)S(1)}, bf16[1024,256]{0,1:T(8,128)(2,1)}, u32[]{:S(2)}) copy-start(bf16[1024,256]{0,1:T(8,128)(2,1)} %get-tuple-element.7) | copy-start | bytes 1572868
  315.8 4.5 %copy-start.9 = (bf16[1,2048,256]{2,1,0:T(8,128)(2,1)S(1)}, bf16[1,2048,256]{2,1,0:T(8,128)(2,1)}, u32[]{:S(2)}) copy-start(bf16[1,2048,256]{2,1,0:T(8,128)(2,1)} %fusion.15) | copy-start | bytes 3145732
Sparse Core Ops, SparseCore 0:
  31.2 36.9 all-gather.10
  70.1 50.7 all-gather.12
  148.4 23.5 all-gather.6
  173.7 51.7 all-gather.8
where the time goes:
time: 332 us; the launch traced here: 328 us
  waiting for transfers between devices  227 us (68%)
  starting transfers between devices  24.5 us (7%)
  local copies, waits for them, and re-layouts  18.9 us (6%)
  matrix products  15.3 us (5%)
  blocking collectives  14.6 us (4%)
  other arithmetic  14.2 us (4%)
  between operations  14 us (4%)
    all_gather x4, waiting for transfers between devices, whole_of(): x = lax.all_gather(x, axis, axis=dim, tiled=True)  144 us
    all_to_all x1, waiting for transfers between devices, summed_on_arrival(): pieces = lax.all_to_all(cut_along(x, dim, length), axis, 0, 0, tiled=True)  54.3 us
    all_to_all x1, waiting for transfers between devices, shards(): lax.all_to_all(outgoing, 'group', split_axis=0, concat_axis=2, tiled=True)  18.6 us
    psum x1, blocking collectives, shards(): inner = lax.psum(jnp.sum(normed_grad * middle, axis=-1), MP)  14.6 us
    unnamed x35, local copies, waits for them, and re-layouts  14.5 us
    all_to_all x1, starting transfers between devices, shards(): lax.all_to_all(deltas.astype(jnp.bfloat16), 'group', split_axis=2, concat...  12.9 us
    all_to_all x1, waiting for transfers between devices, shards(): lax.all_to_all(deltas.astype(jnp.bfloat16), 'group', split_axis=2, concat...  9.6 us
  transfers between devices with their start and end apart: 7, of which 7 were waited for; matrix products, arithmetic and copies ran while one was open for 5% of the time, Pallas kernels for 0%

commit v1 on v0

v1 whole, which is shorter than its diff:
```python
import math

import jax
import jax.numpy as jnp
from jax import lax
from jax.experimental import pallas as pl
from jax.experimental.pallas import tpu as pltpu
from jax.sharding import Mesh
from jax.sharding import PartitionSpec as P

D = 2048
MODS = 8
GROUPS = 32
ROWS = 1024
LEVELS = 2
BLOCK = D // GROUPS
WIDTH = 256
PARTS = D // WIDTH
CHUNKS = 4
CHUNK = ROWS // CHUNKS
HALF = CHUNK // 2
TILE = 16
FACTOR = 1.0 / math.sqrt(D)

outer_rate = 0.7
momentum_rate = 0.9
epsilon = 1e-06

AXES = ("z", "yh", "c", "x", "yl")
SIZES = (8, 2, 2, 4, 2)
GROUP = ("z", "yh", "c")
MP = ("x", "yl")
NEAR = (3, -3, 2, -2, 1, -1, 0)
RELAYS = 18
BF16 = jnp.bfloat16
F32 = jnp.float32


def wrap(value, size):
    return lax.rem(value + size, size)


def sigmoid(values):
    return 1.0 / (1.0 + jnp.exp(-values))


def silu_slope(values):
    part = sigmoid(values)
    return part * (1.0 + values * (1.0 - part))


def dot(a, b, dims):
    return lax.dot_general(a, b, ((dims[0:1], dims[1:2]), ((), ())), preferred_element_type=F32)


def kernel(
    old_ref,
    new_ref,
    anchor_ref,
    momentum_ref,
    deltas_ref,
    tokens_ref,
    cot_ref,
    out_anchor,
    out_momentum,
    out_grads,
    raw,
    send,
    recv,
    relay,
    anchor,
    momentum,
    modules,
    tok,
    cot,
    state,
    pre0,
    scale0,
    scale1,
    slopes,
    terms,
    ra,
    rb,
    rc,
    inner,
    acc,
    gout,
    load_sem,
    store_sem,
    send_sem,
    relay_sem,
    recv_sem,
    tok_sem,
    state_sem,
    rs_sem,
    inner_sem,
):
    z = lax.axis_index("z")
    yh = lax.axis_index("yh")
    c = lax.axis_index("c")
    x = lax.axis_index("x")
    yl = lax.axis_index("yl")
    y = yh * 2 + yl
    group = z * 4 + yh * 2 + c
    mine = x * 2 + yl

    def remote(src, dst, sender, receiver, device):
        return pltpu.make_async_remote_copy(
            src_ref=src,
            dst_ref=dst,
            send_sem=sender,
            recv_sem=receiver,
            device_id=device,
            device_id_type=pl.DeviceIdType.MESH,
        )

    def wait_bytes(ref, sem):
        pltpu.make_async_copy(ref, ref, sem).wait()

    def place(dz, dy, core):
        there = wrap(y + dy, 4)
        return (wrap(z + dz, 8), there // 2, core, x, lax.rem(there, 2))

    def send_blocks(p):
        def go(dz, cross, core, dst, receiver, device):
            target = wrap(z + dz, 8) * 4 + lax.rem(yh + cross, 2) * 2 + core
            remote(send.at[p, target], dst, send_sem.at[p], receiver, device).start()

        for i, sign in enumerate((1, -1)):
            go(4, 1, i, relay.at[p, 14 + i], relay_sem.at[p, 14 + i], place(2 * sign, sign, c))
            go(4, 0, i, relay.at[p, 16 + i], relay_sem.at[p, 16 + i], place(2 * sign, 0, c))
        for j, dz in enumerate(NEAR):
            for i, sign in enumerate((1, -1)):
                slot = i * 7 + j
                go(dz, 1, i, relay.at[p, slot], relay_sem.at[p, slot], place(dz, sign, c))
        for dz in NEAR:
            if dz == 0:
                go(0, 0, 1 - c, recv.at[p, group], recv_sem.at[p], place(0, 0, 1 - c))
            else:
                for i in range(2):
                    go(dz, 0, i, recv.at[p, group], recv_sem.at[p], place(dz, 0, i))

    def forward_blocks(p):
        def go(slot, dz, dy, device):
            source = wrap(z - dz, 8) * 4 + (wrap(y - dy, 4) // 2) * 2 + c
            wait_bytes(relay.at[p, slot], relay_sem.at[p, slot])
            remote(
                relay.at[p, slot], recv.at[p, source], send_sem.at[4 + p], recv_sem.at[p], device
            ).start()

        for i, sign in enumerate((1, -1)):
            go(14 + i, 2 * sign, sign, place(2 * sign, sign, i))
            go(16 + i, 2 * sign, 0, place(2 * sign, 0, i))
        for j, dz in enumerate(NEAR):
            for i, sign in enumerate((1, -1)):
                go(i * 7 + j, dz, sign, place(0, sign, i))

    def update(l):
        wait_bytes(recv.at[l, pl.ds(0, GROUPS - 1)], recv_sem.at[l])

        def count_one(g, counts):
            named = old_ref[g, l]
            return tuple(n + jnp.where(named == m, 1.0, 0.0) for m, n in enumerate(counts))

        counts = lax.fori_loop(0, GROUPS, count_one, (jnp.float32(0.0),) * MODS)

        def rows_of(r, carry):
            rows = pl.ds(pl.multiple_of(r * TILE, TILE), TILE)

            def add_one(g, sums):
                named = old_ref[g, l]
                value = recv[l, g, rows, :].astype(F32)
                return tuple(
                    s + value * jnp.where(named == m, 1.0, 0.0) for m, s in enumerate(sums)
                )

            sums = lax.fori_loop(
                0, GROUPS, add_one, (jnp.zeros((TILE, WIDTH), F32),) * MODS
            )
            for m in range(MODS):
                k = l * MODS + m
                outer_grad = sums[m] / counts[m]
                fresh = momentum_rate * momentum[k, rows, :] + outer_grad
                moved = anchor[k, rows, :] - outer_rate * (outer_grad + momentum_rate * fresh)
                momentum[k, rows, :] = fresh
                anchor[k, rows, :] = moved
                modules[k, rows, :] = moved.astype(BF16)
            return carry

        lax.fori_loop(0, BLOCK // TILE, rows_of, 0)

        def stage(g, carry):
            send[2 + l, g] = modules[l * MODS + new_ref[g, l]]
            return carry

        lax.fori_loop(0, GROUPS, stage, 0)
        recv[2 + l, group] = modules[l * MODS + new_ref[group, l]]
        part = pl.ds(l * MODS, MODS)
        pltpu.make_async_copy(anchor.at[part], out_anchor.at[part], store_sem.at[l]).start()
        pltpu.make_async_copy(momentum.at[part], out_momentum.at[part], store_sem.at[2 + l]).start()

    right, left = wrap(x + 1, 4), wrap(x - 1, 4)
    across = wrap(x + 2, 4)
    other = 1 - yl
    to_right = (z, yh, c, right, yl)
    to_left = (z, yh, c, left, yl)
    to_other = (z, yh, c, x, other)

    def rows_at(i):
        return pl.ds(pl.multiple_of(i * CHUNK, CHUNK), CHUNK)

    def upper(i):
        return pl.ds(pl.multiple_of(i * CHUNK, HALF), HALF)

    def lower(i):
        return pl.ds(pl.multiple_of(i * CHUNK + HALF, HALF), HALF)

    class Gather:
        def __init__(self, buffer, sems, sender):
            self.buffer, self.sems, self.sender = buffer, sems, sender

        def push(self, kind, slot, rows, i, device):
            ref = self.buffer.at[slot, rows]
            remote(ref, ref, self.sender, self.sems.at[kind, i], device).start()

        def wait(self, kind, slot, rows, i):
            wait_bytes(self.buffer.at[slot, rows], self.sems.at[kind, i])

        def own(self, i):
            self.push(2, mine, rows_at(i), i, to_other)
            self.push(0, mine, rows_at(i), i, to_right)
            self.push(1, mine, rows_at(i), i, to_left)

        def halves(self, i):
            self.wait(0, left * 2 + yl, rows_at(i), i)
            self.push(3, left * 2 + yl, upper(i), i, to_right)
            self.wait(1, right * 2 + yl, rows_at(i), i)
            self.push(4, right * 2 + yl, lower(i), i, to_left)

        def pair(self, i):
            self.wait(2, x * 2 + other, rows_at(i), i)
            self.push(5, x * 2 + other, rows_at(i), i, to_right)
            self.push(6, x * 2 + other, rows_at(i), i, to_left)

        def far(self, i):
            self.wait(3, across * 2 + yl, upper(i), i)
            self.wait(4, across * 2 + yl, lower(i), i)
            self.push(7, across * 2 + yl, rows_at(i), i, to_other)

        def last(self, i):
            self.wait(5, left * 2 + other, rows_at(i), i)
            self.wait(6, right * 2 + other, rows_at(i), i)
            self.wait(7, across * 2 + other, rows_at(i), i)

    def each_chunk(body):
        def step(i, carry):
            body(i)
            return carry

        lax.fori_loop(0, CHUNKS, step, 0)

    def row_scale(buffer, target, i):
        rows = rows_at(i)
        total = jnp.zeros((CHUNK, WIDTH), F32)
        for k in range(PARTS):
            value = buffer[k, rows, :].astype(F32)
            total = total + value * value
        mean = jnp.sum(total, axis=1, keepdims=True) / D
        target[rows, :] = jnp.broadcast_to(lax.rsqrt(mean + epsilon), (CHUNK, 128))

    def weight(l, k):
        return recv[2 + l, pl.ds(4 * k, 4)].reshape(WIDTH, WIDTH)

    def product(buffer, l, i):
        rows = rows_at(i)
        total = dot(buffer[0, rows, :], weight(l, 0), (1, 0))
        for k in range(1, PARTS):
            total = total + dot(buffer[k, rows, :], weight(l, k), (1, 0))
        return total

    load = [
        pltpu.make_async_copy(deltas_ref.at[0, 0], raw.at[0], load_sem.at[0]),
        pltpu.make_async_copy(deltas_ref.at[0, 1], raw.at[1], load_sem.at[1]),
        pltpu.make_async_copy(tokens_ref.at[0], tok.at[mine], load_sem.at[2]),
        pltpu.make_async_copy(cot_ref.at[0], cot, load_sem.at[3]),
        pltpu.make_async_copy(anchor_ref, anchor, load_sem.at[4]),
        pltpu.make_async_copy(momentum_ref, momentum, load_sem.at[5]),
    ]
    for copy in load:
        copy.start()

    def narrow(l):
        def one(g, carry):
            rows = pl.ds(pl.multiple_of(g * BLOCK, BLOCK), BLOCK)
            send[l, g] = raw[l, rows, :].astype(BF16)
            return carry

        lax.fori_loop(0, GROUPS, one, 0)
        recv[l, group] = send[l, group]

    tokens = Gather(tok, tok_sem, send_sem.at[8])
    states = Gather(state, state_sem, send_sem.at[9])

    load[0].wait()
    narrow(0)
    send_blocks(0)
    load[2].wait()
    each_chunk(tokens.own)
    load[1].wait()
    narrow(1)
    send_blocks(1)
    forward_blocks(0)
    each_chunk(tokens.halves)
    each_chunk(tokens.pair)
    load[4].wait()
    load[5].wait()
    update(0)
    send_blocks(2)
    forward_blocks(1)
    each_chunk(tokens.far)
    update(1)
    send_blocks(3)
    each_chunk(tokens.last)
    each_chunk(lambda i: row_scale(tok, scale0, i))
    load[3].wait()
    forward_blocks(2)
    wait_bytes(recv.at[2, pl.ds(0, GROUPS - 1)], recv_sem.at[2])

    def first(i):
        rows = rows_at(i)
        value = product(tok, 0, i) * (scale0[rows, 0:1] * FACTOR)
        pre0[rows, :] = value
        fresh = tok[mine, rows, :].astype(F32) + value * sigmoid(value)
        state[mine, rows, :] = fresh.astype(BF16)
        states.own(i)

    each_chunk(first)
    forward_blocks(3)
    each_chunk(states.halves)
    each_chunk(states.pair)
    each_chunk(states.far)
    wait_bytes(recv.at[3, pl.ds(0, GROUPS - 1)], recv_sem.at[3])

    def push(kind, src, dst, i, device):
        remote(src, dst, send_sem.at[10], rs_sem.at[kind, i], device).start()

    inner[mine] = jnp.zeros((8, CHUNK), F32)

    def second(i):
        states.last(i)
        rows = rows_at(i)
        row_scale(state, scale1, i)
        scale = scale1[rows, 0:1]
        value = product(state, 1, i) * (scale * FACTOR)
        slope = cot[rows, :].astype(F32) * silu_slope(value)
        narrow_slope = slope.astype(BF16)
        slopes[rows, :] = (slope * scale).astype(BF16)
        for k in range(PARTS):
            term = dot(narrow_slope, weight(1, k), (1, 1)) * FACTOR
            terms[k, rows, :] = term.astype(BF16)
        share = jnp.sum(slope * value, axis=1, keepdims=True)
        flat = jnp.transpose(jnp.broadcast_to(share, (CHUNK, 128)))[0:8, :]
        line = lax.broadcasted_iota(jnp.int32, (8, CHUNK), 0)
        inner[mine] = jnp.where(line == i, flat, inner[mine])
        push(0, terms.at[across * 2 + other, rows], ra.at[0, rows], i, to_other)
        push(1, terms.at[right * 2 + other, rows], ra.at[1, rows], i, to_right)
        push(2, terms.at[left * 2 + other, rows], ra.at[2, rows], i, to_left)

    each_chunk(second)
    for step in range(1, PARTS):
        there = wrap(mine + step, PARTS)
        remote(
            inner.at[mine],
            inner.at[mine],
            send_sem.at[11],
            inner_sem,
            (z, yh, c, there // 2, lax.rem(there, 2)),
        ).start()

    def grad_of(buffer, l, k):
        return dot(buffer[k], slopes[...], (0, 0)) * FACTOR

    def second_grad(k, carry):
        rows = pl.ds(pl.multiple_of(k * WIDTH, WIDTH), WIDTH)
        gout[1, rows, :] = grad_of(state, 1, k).astype(BF16)
        return carry

    def join(i):
        rows = rows_at(i)
        wait_bytes(ra.at[0, rows], rs_sem.at[0, i])
        slot = across * 2 + yl
        total = terms[slot, rows, :].astype(F32) + ra[0, rows, :].astype(F32)
        terms[slot, rows, :] = total.astype(BF16)
        push(3, terms.at[slot, upper(i)], rb.at[0, i], i, to_right)
        push(4, terms.at[slot, lower(i)], rb.at[1, i], i, to_left)

    def meet(i):
        rows = rows_at(i)
        wait_bytes(ra.at[1, rows], rs_sem.at[1, i])
        wait_bytes(ra.at[2, rows], rs_sem.at[2, i])
        slot = x * 2 + other
        total = (
            terms[slot, rows, :].astype(F32)
            + ra[1, rows, :].astype(F32)
            + ra[2, rows, :].astype(F32)
        )
        terms[slot, rows, :] = total.astype(BF16)
        push(7, terms.at[slot, rows], rc.at[2, rows], i, to_other)

    def pass_on(i):
        rows = rows_at(i)
        wait_bytes(rb.at[0, i], rs_sem.at[3, i])
        slot = right * 2 + yl
        total = terms[slot, upper(i), :].astype(F32) + rb[0, i].astype(F32)
        terms[slot, upper(i), :] = total.astype(BF16)
        push(5, terms.at[slot, rows], rc.at[0, rows], i, to_right)
        wait_bytes(rb.at[1, i], rs_sem.at[4, i])
        slot = left * 2 + yl
        total = terms[slot, lower(i), :].astype(F32) + rb[1, i].astype(F32)
        terms[slot, lower(i), :] = total.astype(BF16)
        push(6, terms.at[slot, rows], rc.at[1, rows], i, to_left)

    each_chunk(join)
    lax.fori_loop(0, PARTS, second_grad, 0)
    each_chunk(meet)
    each_chunk(pass_on)
    pltpu.make_async_copy(gout.at[1], out_grads.at[0, 1], store_sem.at[4]).start()
    wait_bytes(inner.at[pl.ds(0, PARTS - 1)], inner_sem)
    acc[...] = jnp.zeros_like(acc)

    def finish(i):
        rows = rows_at(i)
        wait_bytes(rc.at[0, rows], rs_sem.at[5, i])
        wait_bytes(rc.at[1, rows], rs_sem.at[6, i])
        wait_bytes(rc.at[2, rows], rs_sem.at[7, i])
        normed_grad = (
            terms[mine, rows, :].astype(F32)
            + rc[0, rows, :].astype(F32)
            + rc[1, rows, :].astype(F32)
            + rc[2, rows, :].astype(F32)
        )
        line = lax.broadcasted_iota(jnp.int32, (8, CHUNK), 0)
        total = inner[0]
        for k in range(1, PARTS):
            total = total + inner[k]
        flat = jnp.sum(jnp.where(line == i, total, 0.0), axis=0, keepdims=True)
        share = jnp.transpose(jnp.broadcast_to(flat, (128, CHUNK)))[:, 0:1]
        scale = scale1[rows, 0:1]
        state_grad = (
            cot[rows, :].astype(F32)
            + scale * normed_grad
            - state[mine, rows, :].astype(F32) * (scale * scale * share / D)
        )
        slope = state_grad * silu_slope(pre0[rows, :])
        narrow_slope = (slope * scale0[rows, 0:1]).astype(BF16)
        for k in range(PARTS):
            acc[k] += dot(tok[k, rows, :], narrow_slope, (0, 0))

    each_chunk(finish)

    def first_grad(k, carry):
        rows = pl.ds(pl.multiple_of(k * WIDTH, WIDTH), WIDTH)
        gout[0, rows, :] = (acc[k] * FACTOR).astype(BF16)
        return carry

    lax.fori_loop(0, PARTS, first_grad, 0)
    pltpu.make_async_copy(gout.at[0], out_grads.at[0, 0], store_sem.at[5]).start()

    for p in range(4):
        wait_bytes(send.at[p, pl.ds(0, GROUPS - 1)], send_sem.at[p])
        wait_bytes(relay.at[p], send_sem.at[4 + p])
    wait_bytes(tok.at[pl.ds(0, PARTS - 1)], send_sem.at[8])
    wait_bytes(state.at[pl.ds(0, PARTS - 1)], send_sem.at[9])
    wait_bytes(terms.at[pl.ds(0, PARTS - 1)], send_sem.at[10])
    wait_bytes(inner.at[pl.ds(0, PARTS - 1)], send_sem.at[11])
    for l in range(LEVELS):
        part = pl.ds(l * MODS, MODS)
        pltpu.make_async_copy(anchor.at[part], out_anchor.at[part], store_sem.at[l]).wait()
        pltpu.make_async_copy(momentum.at[part], out_momentum.at[part], store_sem.at[2 + l]).wait()
    pltpu.make_async_copy(gout.at[1], out_grads.at[0, 1], store_sem.at[4]).wait()
    pltpu.make_async_copy(gout.at[0], out_grads.at[0, 0], store_sem.at[5]).wait()


def shards(anchor, momentum, deltas, old_path, new_path, tokens, cotangent):
    anywhere = pl.BlockSpec(memory_space=pl.ANY)
    scalars = pl.BlockSpec(memory_space=pltpu.SMEM)
    dma = pltpu.SemaphoreType.DMA
    return pl.pallas_call(
        kernel,
        out_shape=(
            jax.ShapeDtypeStruct(anchor.shape, F32),
            jax.ShapeDtypeStruct(momentum.shape, F32),
            jax.ShapeDtypeStruct((1, LEVELS, D, WIDTH), BF16),
        ),
        in_specs=[scalars, scalars] + [anywhere] * 5,
        out_specs=(anywhere,) * 3,
        scratch_shapes=[
            pltpu.VMEM((LEVELS, D, WIDTH), F32),
            pltpu.VMEM((4, GROUPS, BLOCK, WIDTH), BF16),
            pltpu.VMEM((4, GROUPS, BLOCK, WIDTH), BF16),
            pltpu.VMEM((4, RELAYS, BLOCK, WIDTH), BF16),
            pltpu.VMEM((LEVELS * MODS, BLOCK, WIDTH), F32),
            pltpu.VMEM((LEVELS * MODS, BLOCK, WIDTH), F32),
            pltpu.VMEM((LEVELS * MODS, BLOCK, WIDTH), BF16),
            pltpu.VMEM((PARTS, ROWS, WIDTH), BF16),
            pltpu.VMEM((ROWS, WIDTH), BF16),
            pltpu.VMEM((PARTS, ROWS, WIDTH), BF16),
            pltpu.VMEM((ROWS, WIDTH), F32),
            pltpu.VMEM((ROWS, 128), F32),
            pltpu.VMEM((ROWS, 128), F32),
            pltpu.VMEM((ROWS, WIDTH), BF16),
            pltpu.VMEM((PARTS, ROWS, WIDTH), BF16),
            pltpu.VMEM((3, ROWS, WIDTH), BF16),
            pltpu.VMEM((2, CHUNKS, HALF, WIDTH), BF16),
            pltpu.VMEM((3, ROWS, WIDTH), BF16),
            pltpu.VMEM((PARTS, 8, CHUNK), F32),
            pltpu.VMEM((PARTS, WIDTH, WIDTH), F32),
            pltpu.VMEM((LEVELS, D, WIDTH), BF16),
            dma((6,)),
            dma((6,)),
            dma((12,)),
            dma((4, RELAYS)),
            dma((4,)),
            dma((8, CHUNKS)),
            dma((8, CHUNKS)),
            dma((8, CHUNKS)),
            dma(()),
        ],
        compiler_params=pltpu.CompilerParams(
            has_side_effects=True, vmem_limit_bytes=62 * 1024 * 1024
        ),
    )(old_path, new_path, anchor, momentum, deltas, tokens, cotangent)


def solution(mesh):
    split = Mesh(mesh.devices.reshape(SIZES), AXES)
    placed = (
        P(None, GROUP, MP),
        P(None, GROUP, MP),
        P(GROUP, None, None, MP),
        P(),
        P(),
        P(GROUP, None, MP),
        P(GROUP, None, MP),
    )
    return jax.shard_map(
        shards,
        mesh=split,
        in_specs=placed,
        out_specs=(P(None, GROUP, MP), P(None, GROUP, MP), P(GROUP, None, None, MP)),
        check_vma=False,
    )
```

time: 332 us -> 194 us (0.58)
  waiting for transfers between devices: 227 us -> 0 us
  Pallas kernels: 0 us -> 185 us
  starting transfers between devices: 24.5 us -> 0 us
  matrix products: 15.3 us -> 0 us
  blocking collectives: 14.6 us -> 0 us
  other arithmetic: 14.2 us -> 0 us
  between operations: 14 us -> 0.66 us
  local copies, waits for them, and re-layouts: 18.9 us -> 7.47 us
    pallas_call x0 -> x1, Pallas kernels: none -> 185 us  [shards(): pl.pallas_call(kernel, out_shape=(jax.ShapeDtypeStruct(anchor.shape, F32)...]
    all_gather x4 -> x0, waiting for transfers between devices: 144 us -> none  [whole_of(): x = lax.all_gather(x, axis, axis=dim, tiled=True)]
    all_to_all x3 -> x0, waiting for transfers between devices: 82.5 us -> none  [the longest x1 54.3 us: summed_on_arrival(): pieces = lax.all_to_all(cut_along(x, dim, length), axis, 0, 0, tiled=True)]
    all_to_all x3 -> x0, starting transfers between devices: 24.1 us -> none  [the longest x1 12.9 us: shards(): lax.all_to_all(deltas.astype(jnp.bfloat16), 'group', split_axis=2, concat...]
    dot_general x6 -> x0, matrix products: 15.3 us -> none  [the longest x1 4.63 us: shards(): lax.dot_general(second_normed, second_slope, (((0,), (0,)), ((), ())), pr...]
    psum x1 -> x0, blocking collectives: 14.6 us -> none  [shards(): inner = lax.psum(jnp.sum(normed_grad * middle, axis=-1), MP)]
    reduce_sum x5 -> x0, other arithmetic: 9.47 us -> none  [the longest x2 6.34 us: normalize(): scale = lax.rsqrt(jnp.mean(values * values, axis=-1) + epsilon)]
    unnamed x35 -> x9, local copies, waits for them, and re-layouts: 14.5 us -> 7.47 us
  transfers between devices with their start and end apart: 7 -> 0, of which waited for: 7 -> 0; matrix products, arithmetic and copies ran while one was open for 5% -> 0% of each run, Pallas kernels for 0% -> 0%
where the time goes in v1:
time: 194 us
  Pallas kernels  185 us (95%)
  local copies, waits for them, and re-layouts  7.47 us (4%)
    pallas_call x1, Pallas kernels, shards(): pl.pallas_call(kernel, out_shape=(jax.ShapeDtypeStruct(anchor.shape, F32)...  185 us
    unnamed x9, local copies, waits for them, and re-layouts  7.47 us

profile of v1, /device:TPU:1, one launch (start us, length us, event | category | flops | bytes accessed | tf_op | source)
XLA Modules:
  0.0 193.6 jit_solution(956771805553184916)
XLA Ops:
  0.6 1.4 copy.10.old_ref
  2.0 1.4 copy.11.new_ref
  3.4 185.4 %shard_map.94 = (f32[16,64,256]{2,1,0:T(8,128)}, f32[16,64,256]{2,1,0:T(8,128)}, bf16[1,2,2048,256]{3,2,1,0:T(8,128)(2,1)}) custom-call(s32[32,2]{1,0:T(8,128)} %copy.10.old_ref, s32[32,2]{1,0:T(8,128)} %copy.11.new_ref, f32[16,64,256]{2,1,0:T(8,128)} %anchor_ref.1, f32[16,64,256]{2,1,0:T(8,128)} %momentum_ref.1, f32[1,2,2048,256]{3,2,1,0:T(8,128)} %deltas_ref.1, ...), custom_call_target="tpu_custom_call" | custom-call | tf_op jit(solution)/shard_map/pallas_call | solution.py:488
  188.8 0.0 copy-start.1
  188.8 0.0 copy-start
  188.8 2.4 %copy.15 = f32[16,64,256]{2,1,0:T(8,128)} copy(f32[16,64,256]{2,1,0:T(8,128)} %get-tuple-element.6) | data formatting | bytes 2097152
  191.3 0.0 copy-done.1
  191.3 1.0 copy.16
  192.2 0.0 copy-done
  192.2 1.3 copy.17
Async XLA Ops:
  188.8 2.5 %copy-start.1 = (f32[16,64,256]{2,1,0:T(8,128)S(1)}, f32[16,64,256]{2,1,0:T(8,128)}, u32[]{:S(2)}) copy-start(f32[16,64,256]{2,1,0:T(8,128)} %get-tuple-element.7) | copy-start | bytes 3145732
  188.8 3.4 %copy-start = (bf16[1,2,2048,256]{3,2,1,0:T(8,128)(2,1)S(1)}, bf16[1,2,2048,256]{3,2,1,0:T(8,128)(2,1)}, u32[]{:S(2)}) copy-start(bf16[1,2,2048,256]{3,2,1,0:T(8,128)(2,1)} %get-tuple-element.8) | copy-start | bytes 6291460

commit v2 on v1

--- a/solution.py
+++ b/solution.py
@@ -20,6 +20,7 @@
 CHUNK = ROWS // CHUNKS
 HALF = CHUNK // 2
 TILE = 16
+SPAN = 8
 FACTOR = 1.0 / math.sqrt(D)
 
 outer_rate = 0.7
@@ -61,15 +62,13 @@
     deltas_ref,
     tokens_ref,
     cot_ref,
-    out_anchor,
-    out_momentum,
-    out_grads,
+    anchor,
+    momentum,
+    grads,
     raw,
     send,
     recv,
     relay,
-    anchor,
-    momentum,
     modules,
     tok,
     cot,
@@ -84,9 +83,7 @@
     rc,
     inner,
     acc,
-    gout,
     load_sem,
-    store_sem,
     send_sem,
     relay_sem,
     recv_sem,
@@ -121,24 +118,43 @@
         there = wrap(y + dy, 4)
         return (wrap(z + dz, 8), there // 2, core, x, lax.rem(there, 2))
 
-    def send_blocks(p):
-        def go(dz, cross, core, dst, receiver, device):
-            target = wrap(z + dz, 8) * 4 + lax.rem(yh + cross, 2) * 2 + core
-            remote(send.at[p, target], dst, send_sem.at[p], receiver, device).start()
+    partners = [place(0, 0, 1 - c)]
+    for dz in NEAR:
+        if dz != 0:
+            partners += [place(dz, 0, 0), place(dz, 0, 1)]
+        for dy in (1, -1):
+            partners.append(place(dz, dy, c))
+            if dz in (0, 2, -2):
+                partners.append(place(dz, dy, 1 - c))
+    for dx in (1, 2, 3):
+        for part in (yl, 1 - yl):
+            partners.append((z, yh, c, wrap(x + dx, 4), part))
+    barrier = pltpu.get_barrier_semaphore()
+    for partner in partners:
+        pl.semaphore_signal(
+            barrier, inc=1, device_id=partner, device_id_type=pl.DeviceIdType.MESH
+        )
+
+    def send_block(p, dz, cross, core, dst, receiver, device):
+        target = wrap(z + dz, 8) * 4 + lax.rem(yh + cross, 2) * 2 + core
+        remote(send.at[p, target], dst, send_sem.at[p], receiver, device).start()
+
+    def send_relayed(p):
+        def go(dz, cross, core, slot, device):
+            send_block(p, dz, cross, core, relay.at[p, slot], relay_sem.at[p, slot], device)
 
         for i, sign in enumerate((1, -1)):
-            go(4, 1, i, relay.at[p, 14 + i], relay_sem.at[p, 14 + i], place(2 * sign, sign, c))
-            go(4, 0, i, relay.at[p, 16 + i], relay_sem.at[p, 16 + i], place(2 * sign, 0, c))
+            go(4, 1, i, 14 + i, place(2 * sign, sign, c))
+            go(4, 0, i, 16 + i, place(2 * sign, 0, c))
         for j, dz in enumerate(NEAR):
             for i, sign in enumerate((1, -1)):
-                slot = i * 7 + j
-                go(dz, 1, i, relay.at[p, slot], relay_sem.at[p, slot], place(dz, sign, c))
+                go(dz, 1, i, i * 7 + j, place(dz, sign, c))
+
+    def send_direct(p):
         for dz in NEAR:
-            if dz == 0:
-                go(0, 0, 1 - c, recv.at[p, group], recv_sem.at[p], place(0, 0, 1 - c))
-            else:
-                for i in range(2):
-                    go(dz, 0, i, recv.at[p, group], recv_sem.at[p], place(dz, 0, i))
+            for core in (1 - c,) if dz == 0 else (0, 1):
+                device = place(dz, 0, core)
+                send_block(p, dz, 0, core, recv.at[p, group], recv_sem.at[p], device)
 
     def forward_blocks(p):
         def go(slot, dz, dy, device):
@@ -159,7 +175,7 @@
         wait_bytes(recv.at[l, pl.ds(0, GROUPS - 1)], recv_sem.at[l])
 
         def count_one(g, counts):
-            named = old_ref[g, l]
+            named = old_ref[l, g]
             return tuple(n + jnp.where(named == m, 1.0, 0.0) for m, n in enumerate(counts))
 
         counts = lax.fori_loop(0, GROUPS, count_one, (jnp.float32(0.0),) * MODS)
@@ -167,15 +183,18 @@
         def rows_of(r, carry):
             rows = pl.ds(pl.multiple_of(r * TILE, TILE), TILE)
 
-            def add_one(g, sums):
-                named = old_ref[g, l]
-                value = recv[l, g, rows, :].astype(F32)
-                return tuple(
-                    s + value * jnp.where(named == m, 1.0, 0.0) for m, s in enumerate(sums)
-                )
+            def add_some(step, sums):
+                for j in range(SPAN):
+                    g = step * SPAN + j
+                    named = old_ref[l, g]
+                    value = recv[l, g, rows, :].astype(F32)
+                    sums = tuple(
+                        s + value * jnp.where(named == m, 1.0, 0.0) for m, s in enumerate(sums)
+                    )
+                return sums
 
             sums = lax.fori_loop(
-                0, GROUPS, add_one, (jnp.zeros((TILE, WIDTH), F32),) * MODS
+                0, GROUPS // SPAN, add_some, (jnp.zeros((TILE, WIDTH), F32),) * MODS
             )
             for m in range(MODS):
                 k = l * MODS + m
@@ -190,14 +209,11 @@
         lax.fori_loop(0, BLOCK // TILE, rows_of, 0)
 
         def stage(g, carry):
-            send[2 + l, g] = modules[l * MODS + new_ref[g, l]]
+            send[2 + l, g] = modules[l * MODS + new_ref[l, g]]
             return carry
 
         lax.fori_loop(0, GROUPS, stage, 0)
-        recv[2 + l, group] = modules[l * MODS + new_ref[group, l]]
-        part = pl.ds(l * MODS, MODS)
-        pltpu.make_async_copy(anchor.at[part], out_anchor.at[part], store_sem.at[l]).start()
-        pltpu.make_async_copy(momentum.at[part], out_momentum.at[part], store_sem.at[2 + l]).start()
+        recv[2 + l, group] = modules[l * MODS + new_ref[l, group]]
 
     right, left = wrap(x + 1, 4), wrap(x - 1, 4)
     across = wrap(x + 2, 4)
@@ -303,27 +319,29 @@
 
     load[0].wait()
     narrow(0)
-    send_blocks(0)
+    pl.semaphore_wait(barrier, len(partners))
+    send_relayed(0)
+    send_direct(0)
     load[2].wait()
     each_chunk(tokens.own)
     load[1].wait()
     narrow(1)
-    send_blocks(1)
     forward_blocks(0)
+    send_relayed(1)
     each_chunk(tokens.halves)
     each_chunk(tokens.pair)
+    each_chunk(tokens.far)
     load[4].wait()
     load[5].wait()
     update(0)
-    send_blocks(2)
+    send_relayed(2)
+    send_direct(2)
     forward_blocks(1)
-    each_chunk(tokens.far)
-    update(1)
-    send_blocks(3)
+    forward_blocks(2)
+    send_direct(1)
     each_chunk(tokens.last)
     each_chunk(lambda i: row_scale(tok, scale0, i))
     load[3].wait()
-    forward_blocks(2)
     wait_bytes(recv.at[2, pl.ds(0, GROUPS - 1)], recv_sem.at[2])
 
     def first(i):
@@ -335,10 +353,19 @@
         states.own(i)
 
     each_chunk(first)
-    forward_blocks(3)
+    update(1)
+    send_relayed(3)
+    send_direct(3)
     each_chunk(states.halves)
     each_chunk(states.pair)
     each_chunk(states.far)
+    forward_blocks(3)
+
+    def gathered(i):
+        states.last(i)
+        row_scale(state, scale1, i)
+
+    each_chunk(gathered)
     wait_bytes(recv.at[3, pl.ds(0, GROUPS - 1)], recv_sem.at[3])
 
     def push(kind, src, dst, i, device):
@@ -347,24 +374,32 @@
     inner[mine] = jnp.zeros((8, CHUNK), F32)
 
     def second(i):
-        states.last(i)
-        rows = rows_at(i)
-        row_scale(state, scale1, i)
+        rows = rows_at(i)
         scale = scale1[rows, 0:1]
         value = product(state, 1, i) * (scale * FACTOR)
         slope = cot[rows, :].astype(F32) * silu_slope(value)
         narrow_slope = slope.astype(BF16)
+
+        def term(slot):
+            product_of = dot(narrow_slope, weight(1, slot), (1, 1)) * FACTOR
+            terms[slot, rows, :] = product_of.astype(BF16)
+
+        outgoing = (
+            (across * 2 + other, to_other),
+            (right * 2 + other, to_right),
+            (left * 2 + other, to_left),
+        )
+        for kind, (slot, device) in enumerate(outgoing):
+            term(slot)
+        for kind, (slot, device) in enumerate(outgoing):
+            push(kind, terms.at[slot, rows], ra.at[kind, rows], i, device)
+        for slot in (across * 2 + yl, x * 2 + other, right * 2 + yl, left * 2 + yl, mine):
+            term(slot)
         slopes[rows, :] = (slope * scale).astype(BF16)
-        for k in range(PARTS):
-            term = dot(narrow_slope, weight(1, k), (1, 1)) * FACTOR
-            terms[k, rows, :] = term.astype(BF16)
         share = jnp.sum(slope * value, axis=1, keepdims=True)
         flat = jnp.transpose(jnp.broadcast_to(share, (CHUNK, 128)))[0:8, :]
         line = lax.broadcasted_iota(jnp.int32, (8, CHUNK), 0)
         inner[mine] = jnp.where(line == i, flat, inner[mine])
-        push(0, terms.at[across * 2 + other, rows], ra.at[0, rows], i, to_other)
-        push(1, terms.at[right * 2 + other, rows], ra.at[1, rows], i, to_right)
-        push(2, terms.at[left * 2 + other, rows], ra.at[2, rows], i, to_left)
 
     each_chunk(second)
     for step in range(1, PARTS):
@@ -382,7 +417,7 @@
 
     def second_grad(k, carry):
         rows = pl.ds(pl.multiple_of(k * WIDTH, WIDTH), WIDTH)
-        gout[1, rows, :] = grad_of(state, 1, k).astype(BF16)
+        grads[0, 1, rows, :] = grad_of(state, 1, k).astype(BF16)
         return carry
 
     def join(i):
@@ -424,7 +459,6 @@
     lax.fori_loop(0, PARTS, second_grad, 0)
     each_chunk(meet)
     each_chunk(pass_on)
-    pltpu.make_async_copy(gout.at[1], out_grads.at[0, 1], store_sem.at[4]).start()
     wait_bytes(inner.at[pl.ds(0, PARTS - 1)], inner_sem)
     acc[...] = jnp.zeros_like(acc)
 
@@ -460,11 +494,10 @@
 
     def first_grad(k, carry):
         rows = pl.ds(pl.multiple_of(k * WIDTH, WIDTH), WIDTH)
-        gout[0, rows, :] = (acc[k] * FACTOR).astype(BF16)
+        grads[0, 0, rows, :] = (acc[k] * FACTOR).astype(BF16)
         return carry
 
     lax.fori_loop(0, PARTS, first_grad, 0)
-    pltpu.make_async_copy(gout.at[0], out_grads.at[0, 0], store_sem.at[5]).start()
 
     for p in range(4):
         wait_bytes(send.at[p, pl.ds(0, GROUPS - 1)], send_sem.at[p])
@@ -473,34 +506,26 @@
     wait_bytes(state.at[pl.ds(0, PARTS - 1)], send_sem.at[9])
     wait_bytes(terms.at[pl.ds(0, PARTS - 1)], send_sem.at[10])
     wait_bytes(inner.at[pl.ds(0, PARTS - 1)], send_sem.at[11])
-    for l in range(LEVELS):
-        part = pl.ds(l * MODS, MODS)
-        pltpu.make_async_copy(anchor.at[part], out_anchor.at[part], store_sem.at[l]).wait()
-        pltpu.make_async_copy(momentum.at[part], out_momentum.at[part], store_sem.at[2 + l]).wait()
-    pltpu.make_async_copy(gout.at[1], out_grads.at[0, 1], store_sem.at[4]).wait()
-    pltpu.make_async_copy(gout.at[0], out_grads.at[0, 0], store_sem.at[5]).wait()
 
 
 def shards(anchor, momentum, deltas, old_path, new_path, tokens, cotangent):
-    anywhere = pl.BlockSpec(memory_space=pl.ANY)
+    anywhere = pl.BlockSpec(memory_space=pltpu.HBM)
     scalars = pl.BlockSpec(memory_space=pltpu.SMEM)
     dma = pltpu.SemaphoreType.DMA
     return pl.pallas_call(
         kernel,
         out_shape=(
-            jax.ShapeDtypeStruct(anchor.shape, F32),
-            jax.ShapeDtypeStruct(momentum.shape, F32),
-            jax.ShapeDtypeStruct((1, LEVELS, D, WIDTH), BF16),
+            pltpu.VMEM(anchor.shape, F32),
+            pltpu.VMEM(momentum.shape, F32),
+            pltpu.VMEM((1, LEVELS, D, WIDTH), BF16),
         ),
         in_specs=[scalars, scalars] + [anywhere] * 5,
-        out_specs=(anywhere,) * 3,
+        out_specs=(pl.BlockSpec(memory_space=pltpu.VMEM),) * 3,
         scratch_shapes=[
             pltpu.VMEM((LEVELS, D, WIDTH), F32),
             pltpu.VMEM((4, GROUPS, BLOCK, WIDTH), BF16),
             pltpu.VMEM((4, GROUPS, BLOCK, WIDTH), BF16),
             pltpu.VMEM((4, RELAYS, BLOCK, WIDTH), BF16),
-            pltpu.VMEM((LEVELS * MODS, BLOCK, WIDTH), F32),
-            pltpu.VMEM((LEVELS * MODS, BLOCK, WIDTH), F32),
             pltpu.VMEM((LEVELS * MODS, BLOCK, WIDTH), BF16),
             pltpu.VMEM((PARTS, ROWS, WIDTH), BF16),
             pltpu.VMEM((ROWS, WIDTH), BF16),
@@ -515,8 +540,6 @@
             pltpu.VMEM((3, ROWS, WIDTH), BF16),
             pltpu.VMEM((PARTS, 8, CHUNK), F32),
             pltpu.VMEM((PARTS, WIDTH, WIDTH), F32),
-            pltpu.VMEM((LEVELS, D, WIDTH), BF16),
-            dma((6,)),
             dma((6,)),
             dma((12,)),
             dma((4, RELAYS)),
@@ -527,9 +550,9 @@
             dma(()),
         ],
         compiler_params=pltpu.CompilerParams(
-            has_side_effects=True, vmem_limit_bytes=62 * 1024 * 1024
+            collective_id=0, has_side_effects=True, vmem_limit_bytes=59 * 1024 * 1024
         ),
-    )(old_path, new_path, anchor, momentum, deltas, tokens, cotangent)
+    )(old_path.T, new_path.T, anchor, momentum, deltas, tokens, cotangent)
 
 
 def solution(mesh):

time: 194 us -> 148 us (0.76)
  Pallas kernels: 185 us -> 144 us
  local copies, waits for them, and re-layouts: 7.47 us -> 3.26 us
    pallas_call x1, Pallas kernels: 185 us -> 144 us  [shards(): pl.pallas_call(kernel, out_shape=(pltpu.VMEM(anchor.shape, F32), pltpu.VM...]
    unnamed x9 -> x3, local copies, waits for them, and re-layouts: 7.47 us -> 3.26 us
where the time goes in v2:
time: 148 us
  Pallas kernels  144 us (97%)
  local copies, waits for them, and re-layouts  3.26 us (2%)
    pallas_call x1, Pallas kernels, shards(): pl.pallas_call(kernel, out_shape=(pltpu.VMEM(anchor.shape, F32), pltpu.VM...  144 us
    unnamed x3, local copies, waits for them, and re-layouts  3.26 us

profile of v2, /device:TPU:1, one launch (start us, length us, event | category | flops | bytes accessed | tf_op | source)
XLA Modules:
  0.0 148.0 jit_solution(13150606891370268269)
XLA Ops:
  0.6 144.1 %shard_map.94 = (f32[16,64,256]{2,1,0:T(8,128)S(1)}, f32[16,64,256]{2,1,0:T(8,128)S(1)}, bf16[1,2,2048,256]{3,2,1,0:T(8,128)(2,1)S(1)}) custom-call(s32[2,32]{1,0:T(2,128)} %bitcast.2, s32[2,32]{1,0:T(2,128)} %bitcast.3, f32[16,64,256]{2,1,0:T(8,128)} %anchor_ref.1, f32[16,64,256]{2,1,0:T(8,128)} %momentum_ref.1, f32[1,2,2048,256]{3,2,1,0:T(8,128)} %deltas_ref.1, ...), custom_call_target="tpu_custom_call" | custom-call | tf_op jit(solution)/shard_map/pallas_call | solution.py:515
  144.7 1.0 copy.13
  145.7 1.0 copy.14
  146.7 1.3 copy.15

commit v3 on v2

--- a/solution.py
+++ b/solution.py
@@ -20,7 +20,8 @@
 CHUNK = ROWS // CHUNKS
 HALF = CHUNK // 2
 TILE = 16
-SPAN = 8
+PIECE = BLOCK // 2
+SPLIT = 1
 FACTOR = 1.0 / math.sqrt(D)
 
 outer_rate = 0.7
@@ -55,8 +56,8 @@
 
 
 def kernel(
-    old_ref,
-    new_ref,
+    old_table,
+    new_table,
     anchor_ref,
     momentum_ref,
     deltas_ref,
@@ -65,11 +66,15 @@
     anchor,
     momentum,
     grads,
+    old_ref,
+    new_ref,
     raw,
     send,
     recv,
     relay,
     modules,
+    selector,
+    count,
     tok,
     cot,
     state,
@@ -101,6 +106,19 @@
     group = z * 4 + yh * 2 + c
     mine = x * 2 + yl
 
+    load = [
+        pltpu.make_async_copy(deltas_ref.at[0, 0], raw.at[0], load_sem.at[0]),
+        pltpu.make_async_copy(deltas_ref.at[0, 1], raw.at[1], load_sem.at[1]),
+        pltpu.make_async_copy(tokens_ref.at[0], tok.at[mine], load_sem.at[2]),
+        pltpu.make_async_copy(cot_ref.at[0], cot, load_sem.at[3]),
+        pltpu.make_async_copy(anchor_ref, anchor, load_sem.at[4]),
+        pltpu.make_async_copy(momentum_ref, momentum, load_sem.at[5]),
+        pltpu.make_async_copy(old_table, old_ref, load_sem.at[6]),
+        pltpu.make_async_copy(new_table, new_ref, load_sem.at[7]),
+    ]
+    for copy in load:
+        copy.start()
+
     def remote(src, dst, sender, receiver, device):
         return pltpu.make_async_remote_copy(
             src_ref=src,
@@ -135,13 +153,17 @@
             barrier, inc=1, device_id=partner, device_id_type=pl.DeviceIdType.MESH
         )
 
-    def send_block(p, dz, cross, core, dst, receiver, device):
+    def piece(h):
+        return pl.ds(0, BLOCK) if h is None else pl.ds(h * PIECE, PIECE)
+
+    def send_block(p, h, dz, cross, core, dst, receiver, device):
         target = wrap(z + dz, 8) * 4 + lax.rem(yh + cross, 2) * 2 + core
-        remote(send.at[p, target], dst, send_sem.at[p], receiver, device).start()
-
-    def send_relayed(p):
+        remote(send.at[p, target, piece(h)], dst, send_sem.at[p], receiver, device).start()
+
+    def send_relayed(p, h=None):
         def go(dz, cross, core, slot, device):
-            send_block(p, dz, cross, core, relay.at[p, slot], relay_sem.at[p, slot], device)
+            dst, receiver = relay.at[p, slot, piece(h)], relay_sem.at[p, h or 0, slot]
+            send_block(p, h, dz, cross, core, dst, receiver, device)
 
         for i, sign in enumerate((1, -1)):
             go(4, 1, i, 14 + i, place(2 * sign, sign, c))
@@ -150,19 +172,19 @@
             for i, sign in enumerate((1, -1)):
                 go(dz, 1, i, i * 7 + j, place(dz, sign, c))
 
-    def send_direct(p):
+    def send_direct(p, h=None):
         for dz in NEAR:
             for core in (1 - c,) if dz == 0 else (0, 1):
-                device = place(dz, 0, core)
-                send_block(p, dz, 0, core, recv.at[p, group], recv_sem.at[p], device)
-
-    def forward_blocks(p):
+                dst, receiver = recv.at[p, group, piece(h)], recv_sem.at[p, 1 + (h or 0)]
+                send_block(p, h, dz, 0, core, dst, receiver, place(dz, 0, core))
+
+    def forward_blocks(p, h=None):
         def go(slot, dz, dy, device):
             source = wrap(z - dz, 8) * 4 + (wrap(y - dy, 4) // 2) * 2 + c
-            wait_bytes(relay.at[p, slot], relay_sem.at[p, slot])
-            remote(
-                relay.at[p, slot], recv.at[p, source], send_sem.at[4 + p], recv_sem.at[p], device
-            ).start()
+            held = relay.at[p, slot, piece(h)]
+            wait_bytes(held, relay_sem.at[p, h or 0, slot])
+            dst = recv.at[p, source, piece(h)]
+            remote(held, dst, send_sem.at[4 + p], recv_sem.at[p, 0], device).start()
 
         for i, sign in enumerate((1, -1)):
             go(14 + i, 2 * sign, sign, place(2 * sign, sign, i))
@@ -171,49 +193,46 @@
             for i, sign in enumerate((1, -1)):
                 go(i * 7 + j, dz, sign, place(0, sign, i))
 
-    def update(l):
-        wait_bytes(recv.at[l, pl.ds(0, GROUPS - 1)], recv_sem.at[l])
-
-        def count_one(g, counts):
-            named = old_ref[l, g]
-            return tuple(n + jnp.where(named == m, 1.0, 0.0) for m, n in enumerate(counts))
-
-        counts = lax.fori_loop(0, GROUPS, count_one, (jnp.float32(0.0),) * MODS)
-
-        def rows_of(r, carry):
-            rows = pl.ds(pl.multiple_of(r * TILE, TILE), TILE)
-
-            def add_some(step, sums):
-                for j in range(SPAN):
-                    g = step * SPAN + j
-                    named = old_ref[l, g]
-                    value = recv[l, g, rows, :].astype(F32)
-                    sums = tuple(
-                        s + value * jnp.where(named == m, 1.0, 0.0) for m, s in enumerate(sums)
-                    )
-                return sums
-
-            sums = lax.fori_loop(
-                0, GROUPS // SPAN, add_some, (jnp.zeros((TILE, WIDTH), F32),) * MODS
-            )
+    def arrive_relayed(p):
+        wait_bytes(recv.at[p, pl.ds(0, RELAYS)], recv_sem.at[p, 0])
+
+    def arrive_direct(p, h=None):
+        near = pl.ds(0, GROUPS - 1 - RELAYS)
+        wait_bytes(recv.at[p, near, piece(h)], recv_sem.at[p, 1 + (h or 0)])
+
+    def prepare(l):
+        tall = (MODS * TILE, GROUPS * TILE)
+        line = lax.broadcasted_iota(jnp.int32, tall, 0)
+        lane = lax.broadcasted_iota(jnp.int32, tall, 1)
+        owner = lax.broadcasted_iota(jnp.int32, (8, GROUPS * TILE), 1) // TILE
+        named = jnp.zeros((8, GROUPS * TILE), jnp.int32)
+        for g in range(GROUPS):
+            named = jnp.where(owner == g, old_ref[l, g], named)
+        wanted = jnp.broadcast_to(named[0:1, :] * TILE, tall) + lane % TILE
+        chosen = jnp.where(line == wanted, 1.0, 0.0)
+        selector[l] = chosen.astype(BF16)
+        count[l] = jnp.broadcast_to(jnp.sum(chosen, axis=1, keepdims=True), (MODS * TILE, 128))
+
+    def update(l, h=None):
+        for r in range(BLOCK // TILE) if h is None else range(2 * h, 2 * h + 2):
+            rows = pl.ds(r * TILE, TILE)
+            values = recv[l, :, rows, :].reshape(GROUPS * TILE, WIDTH)
+            sums = dot(selector[l], values, (1, 0)) / count[l][:, 0:1]
             for m in range(MODS):
                 k = l * MODS + m
-                outer_grad = sums[m] / counts[m]
+                outer_grad = sums[m * TILE : (m + 1) * TILE]
                 fresh = momentum_rate * momentum[k, rows, :] + outer_grad
                 moved = anchor[k, rows, :] - outer_rate * (outer_grad + momentum_rate * fresh)
                 momentum[k, rows, :] = fresh
                 anchor[k, rows, :] = moved
                 modules[k, rows, :] = moved.astype(BF16)
+
+        def stage(g, carry):
+            send[2 + l, g, piece(h), :] = modules[l * MODS + new_ref[l, g], piece(h), :]
             return carry
 
-        lax.fori_loop(0, BLOCK // TILE, rows_of, 0)
-
-        def stage(g, carry):
-            send[2 + l, g] = modules[l * MODS + new_ref[l, g]]
-            return carry
-
-        lax.fori_loop(0, GROUPS, stage, 0)
-        recv[2 + l, group] = modules[l * MODS + new_ref[l, group]]
+        lax.fori_loop(0, GROUPS, stage, 0, unroll=4)
+        recv[2 + l, group, piece(h), :] = modules[l * MODS + new_ref[l, group], piece(h), :]
 
     right, left = wrap(x + 1, 4), wrap(x - 1, 4)
     across = wrap(x + 2, 4)
@@ -263,6 +282,18 @@
             self.wait(4, across * 2 + yl, lower(i), i)
             self.push(7, across * 2 + yl, rows_at(i), i, to_other)
 
+        def far_halves(self, i):
+            self.wait(5, left * 2 + other, rows_at(i), i)
+            self.push(7, left * 2 + other, upper(i), i, to_right)
+            self.wait(6, right * 2 + other, rows_at(i), i)
+            self.push(8, right * 2 + other, lower(i), i, to_left)
+
+        def last_halves(self, i):
+            self.wait(3, across * 2 + yl, upper(i), i)
+            self.wait(4, across * 2 + yl, lower(i), i)
+            self.wait(7, across * 2 + other, upper(i), i)
+            self.wait(8, across * 2 + other, lower(i), i)
+
         def last(self, i):
             self.wait(5, left * 2 + other, rows_at(i), i)
             self.wait(6, right * 2 + other, rows_at(i), i)
@@ -293,17 +324,6 @@
         for k in range(1, PARTS):
             total = total + dot(buffer[k, rows, :], weight(l, k), (1, 0))
         return total
-
-    load = [
-        pltpu.make_async_copy(deltas_ref.at[0, 0], raw.at[0], load_sem.at[0]),
-        pltpu.make_async_copy(deltas_ref.at[0, 1], raw.at[1], load_sem.at[1]),
-        pltpu.make_async_copy(tokens_ref.at[0], tok.at[mine], load_sem.at[2]),
-        pltpu.make_async_copy(cot_ref.at[0], cot, load_sem.at[3]),
-        pltpu.make_async_copy(anchor_ref, anchor, load_sem.at[4]),
-        pltpu.make_async_copy(momentum_ref, momentum, load_sem.at[5]),
-    ]
-    for copy in load:
-        copy.start()
 
     def narrow(l):
         def one(g, carry):
@@ -326,23 +346,31 @@
     each_chunk(tokens.own)
     load[1].wait()
     narrow(1)
+    load[6].wait()
+    load[7].wait()
+    prepare(0)
+    prepare(1)
+    load[4].wait()
+    load[5].wait()
     forward_blocks(0)
     send_relayed(1)
     each_chunk(tokens.halves)
     each_chunk(tokens.pair)
-    each_chunk(tokens.far)
-    load[4].wait()
-    load[5].wait()
+    arrive_relayed(0)
+    arrive_direct(0)
     update(0)
     send_relayed(2)
     send_direct(2)
     forward_blocks(1)
     forward_blocks(2)
-    send_direct(1)
-    each_chunk(tokens.last)
+    send_direct(1, 0)
+    send_direct(1, 1)
+    each_chunk(tokens.far_halves)
+    each_chunk(tokens.last_halves)
     each_chunk(lambda i: row_scale(tok, scale0, i))
     load[3].wait()
-    wait_bytes(recv.at[2, pl.ds(0, GROUPS - 1)], recv_sem.at[2])
+    arrive_relayed(2)
+    arrive_direct(2)
 
     def first(i):
         rows = rows_at(i)
@@ -353,20 +381,32 @@
         states.own(i)
 
     each_chunk(first)
-    update(1)
-    send_relayed(3)
-    send_direct(3)
+    arrive_relayed(1)
+    arrive_direct(1, 0)
+    update(1, 0)
+    send_relayed(3, 0)
+    send_direct(3, 0)
+    arrive_direct(1, 1)
+    update(1, 1)
+    send_relayed(3, 1)
+    send_direct(3, 1)
     each_chunk(states.halves)
+    forward_blocks(3, 0)
     each_chunk(states.pair)
-    each_chunk(states.far)
-    forward_blocks(3)
-
-    def gathered(i):
-        states.last(i)
-        row_scale(state, scale1, i)
-
-    each_chunk(gathered)
-    wait_bytes(recv.at[3, pl.ds(0, GROUPS - 1)], recv_sem.at[3])
+    states.far(1)
+    forward_blocks(3, 1)
+    states.far(2)
+    states.far(3)
+    states.far_halves(0)
+    for i in range(CHUNKS):
+        if i < SPLIT:
+            states.last_halves(i)
+        else:
+            states.last(i)
+    each_chunk(lambda i: row_scale(state, scale1, i))
+    arrive_relayed(3)
+    arrive_direct(3, 0)
+    arrive_direct(3, 1)
 
     def push(kind, src, dst, i, device):
         remote(src, dst, send_sem.at[10], rs_sem.at[kind, i], device).start()
@@ -455,12 +495,27 @@
         terms[slot, lower(i), :] = total.astype(BF16)
         push(6, terms.at[slot, rows], rc.at[1, rows], i, to_left)
 
-    each_chunk(join)
+    each_chunk(lambda i: (join(i), meet(i)))
+    each_chunk(pass_on)
     lax.fori_loop(0, PARTS, second_grad, 0)
-    each_chunk(meet)
-    each_chunk(pass_on)
     wait_bytes(inner.at[pl.ds(0, PARTS - 1)], inner_sem)
     acc[...] = jnp.zeros_like(acc)
+
+    def ready(i):
+        rows = rows_at(i)
+        line = lax.broadcasted_iota(jnp.int32, (8, CHUNK), 0)
+        total = inner[0]
+        for k in range(1, PARTS):
+            total = total + inner[k]
+        flat = jnp.sum(jnp.where(line == i, total, 0.0), axis=0, keepdims=True)
+        share = jnp.transpose(jnp.broadcast_to(flat, (128, CHUNK)))[:, 0:1]
+        scale = scale1[rows, 0:1]
+        raw[0, rows, :] = cot[rows, :].astype(F32) - state[mine, rows, :].astype(F32) * (
+            scale * scale * share / D
+        )
+        raw[1, rows, :] = silu_slope(pre0[rows, :]) * scale0[rows, 0:1]
+
+    each_chunk(ready)
 
     def finish(i):
         rows = rows_at(i)
@@ -473,20 +528,8 @@
             + rc[1, rows, :].astype(F32)
             + rc[2, rows, :].astype(F32)
         )
-        line = lax.broadcasted_iota(jnp.int32, (8, CHUNK), 0)
-        total = inner[0]
-        for k in range(1, PARTS):
-            total = total + inner[k]
-        flat = jnp.sum(jnp.where(line == i, total, 0.0), axis=0, keepdims=True)
-        share = jnp.transpose(jnp.broadcast_to(flat, (128, CHUNK)))[:, 0:1]
-        scale = scale1[rows, 0:1]
-        state_grad = (
-            cot[rows, :].astype(F32)
-            + scale * normed_grad
-            - state[mine, rows, :].astype(F32) * (scale * scale * share / D)
-        )
-        slope = state_grad * silu_slope(pre0[rows, :])
-        narrow_slope = (slope * scale0[rows, 0:1]).astype(BF16)
+        state_grad = raw[0, rows, :] + scale1[rows, 0:1] * normed_grad
+        narrow_slope = (state_grad * raw[1, rows, :]).astype(BF16)
         for k in range(PARTS):
             acc[k] += dot(tok[k, rows, :], narrow_slope, (0, 0))
 
@@ -508,25 +551,40 @@
     wait_bytes(inner.at[pl.ds(0, PARTS - 1)], send_sem.at[11])
 
 
+def store(anchor, momentum, grads, out_anchor, out_momentum, out_grads, sem):
+    copies = [
+        pltpu.make_async_copy(anchor, out_anchor, sem.at[0]),
+        pltpu.make_async_copy(momentum, out_momentum, sem.at[1]),
+        pltpu.make_async_copy(grads, out_grads, sem.at[2]),
+    ]
+    for copy in copies:
+        copy.start()
+    for copy in copies:
+        copy.wait()
+
+
 def shards(anchor, momentum, deltas, old_path, new_path, tokens, cotangent):
     anywhere = pl.BlockSpec(memory_space=pltpu.HBM)
-    scalars = pl.BlockSpec(memory_space=pltpu.SMEM)
     dma = pltpu.SemaphoreType.DMA
-    return pl.pallas_call(
+    held = pl.pallas_call(
         kernel,
         out_shape=(
             pltpu.VMEM(anchor.shape, F32),
             pltpu.VMEM(momentum.shape, F32),
             pltpu.VMEM((1, LEVELS, D, WIDTH), BF16),
         ),
-        in_specs=[scalars, scalars] + [anywhere] * 5,
+        in_specs=[anywhere] * 7,
         out_specs=(pl.BlockSpec(memory_space=pltpu.VMEM),) * 3,
         scratch_shapes=[
+            pltpu.SMEM((LEVELS, GROUPS), jnp.int32),
+            pltpu.SMEM((LEVELS, GROUPS), jnp.int32),
             pltpu.VMEM((LEVELS, D, WIDTH), F32),
             pltpu.VMEM((4, GROUPS, BLOCK, WIDTH), BF16),
             pltpu.VMEM((4, GROUPS, BLOCK, WIDTH), BF16),
             pltpu.VMEM((4, RELAYS, BLOCK, WIDTH), BF16),
             pltpu.VMEM((LEVELS * MODS, BLOCK, WIDTH), BF16),
+            pltpu.VMEM((LEVELS, MODS * TILE, GROUPS * TILE), BF16),
+            pltpu.VMEM((LEVELS, MODS * TILE, 128), F32),
             pltpu.VMEM((PARTS, ROWS, WIDTH), BF16),
             pltpu.VMEM((ROWS, WIDTH), BF16),
             pltpu.VMEM((PARTS, ROWS, WIDTH), BF16),
@@ -540,12 +598,12 @@
             pltpu.VMEM((3, ROWS, WIDTH), BF16),
             pltpu.VMEM((PARTS, 8, CHUNK), F32),
             pltpu.VMEM((PARTS, WIDTH, WIDTH), F32),
-            dma((6,)),
+            dma((8,)),
             dma((12,)),
-            dma((4, RELAYS)),
-            dma((4,)),
-            dma((8, CHUNKS)),
-            dma((8, CHUNKS)),
+            dma((4, 2, RELAYS)),
+            dma((4, 3)),
+            dma((9, CHUNKS)),
+            dma((9, CHUNKS)),
             dma((8, CHUNKS)),
             dma(()),
         ],
@@ -553,6 +611,14 @@
             collective_id=0, has_side_effects=True, vmem_limit_bytes=59 * 1024 * 1024
         ),
     )(old_path.T, new_path.T, anchor, momentum, deltas, tokens, cotangent)
+    return pl.pallas_call(
+        store,
+        out_shape=tuple(jax.ShapeDtypeStruct(part.shape, part.dtype) for part in held),
+        in_specs=[pl.BlockSpec(memory_space=pltpu.VMEM)] * 3,
+        out_specs=(anywhere,) * 3,
+        scratch_shapes=[dma((3,))],
+        compiler_params=pltpu.CompilerParams(vmem_limit_bytes=16 * 1024 * 1024),
+    )(*held)
 
 
 def solution(mesh):

time: 148 us -> 145 us (0.980)
  local copies, waits for them, and re-layouts: 3.26 us -> 0 us
    unnamed x3 -> x0, local copies, waits for them, and re-layouts: 3.26 us -> none
    pallas_call x0 -> x1, Pallas kernels: none -> 2.04 us  [shards(): pl.pallas_call(store, out_shape=tuple((jax.ShapeDtypeStruct(part.shape, p...]
where the time goes in v3:
time: 145 us
  Pallas kernels  145 us (100%)
    pallas_call x1, Pallas kernels, shards(): pl.pallas_call(kernel, out_shape=(pltpu.VMEM(anchor.shape, F32), pltpu.VM...  143 us

profile of v3, /device:TPU:1, one launch (start us, length us, event | category | flops | bytes accessed | tf_op | source)
XLA Modules:
  0.0 145.4 jit_solution(11417703159804482564)
XLA Ops:
  0.6 142.7 %shard_map.94 = (f32[16,64,256]{2,1,0:T(8,128)S(1)}, f32[16,64,256]{2,1,0:T(8,128)S(1)}, bf16[1,2,2048,256]{3,2,1,0:T(8,128)(2,1)S(1)}) custom-call(s32[2,32]{1,0:T(2,128)} %bitcast.2, s32[2,32]{1,0:T(2,128)} %bitcast.3, f32[16,64,256]{2,1,0:T(8,128)} %anchor_ref.1, f32[16,64,256]{2,1,0:T(8,128)} %momentum_ref.1, f32[1,2,2048,256]{3,2,1,0:T(8,128)} %deltas_ref.1, ...), custom_call_target="tpu_custom_call" | custom-call | tf_op jit(solution)/shard_map/pallas_call | solution.py:569
  143.3 2.0 %shard_map.95 = (f32[16,64,256]{2,1,0:T(8,128)}, f32[16,64,256]{2,1,0:T(8,128)}, bf16[1,2,2048,256]{3,2,1,0:T(8,128)(2,1)}) custom-call(f32[16,64,256]{2,1,0:T(8,128)S(1)} %get-tuple-element.6.anchor, f32[16,64,256]{2,1,0:T(8,128)S(1)} %get-tuple-element.7.momentum, bf16[1,2,2048,256]{3,2,1,0:T(8,128)(2,1)S(1)} %get-tuple-element.8.grads), custom_call_target="tpu_custom_call" | custom-call | tf_op jit(solution)/shard_map/pallas_call | solution.py:614

commit v4 on v3

--- a/solution.py
+++ b/solution.py
@@ -86,6 +86,7 @@
     ra,
     rb,
     rc,
+    rd,
     inner,
     acc,
     load_sem,
@@ -299,12 +300,12 @@
             self.wait(6, right * 2 + other, rows_at(i), i)
             self.wait(7, across * 2 + other, rows_at(i), i)
 
-    def each_chunk(body):
+    def each_chunk(body, start=0):
         def step(i, carry):
             body(i)
             return carry
 
-        lax.fori_loop(0, CHUNKS, step, 0)
+        lax.fori_loop(start, CHUNKS, step, 0)
 
     def row_scale(buffer, target, i):
         rows = rows_at(i)
@@ -413,7 +414,7 @@
 
     inner[mine] = jnp.zeros((8, CHUNK), F32)
 
-    def second(i):
+    def second(i, detour=False):
         rows = rows_at(i)
         scale = scale1[rows, 0:1]
         value = product(state, 1, i) * (scale * FACTOR)
@@ -432,7 +433,8 @@
         for kind, (slot, device) in enumerate(outgoing):
             term(slot)
         for kind, (slot, device) in enumerate(outgoing):
-            push(kind, terms.at[slot, rows], ra.at[kind, rows], i, device)
+            part = upper(i) if detour and kind > 0 else rows
+            push(kind, terms.at[slot, part], ra.at[kind, part], i, device)
         for slot in (across * 2 + yl, x * 2 + other, right * 2 + yl, left * 2 + yl, mine):
             term(slot)
         slopes[rows, :] = (slope * scale).astype(BF16)
@@ -441,7 +443,10 @@
         line = lax.broadcasted_iota(jnp.int32, (8, CHUNK), 0)
         inner[mine] = jnp.where(line == i, flat, inner[mine])
 
-    each_chunk(second)
+    second(0, detour=True)
+    each_chunk(second, 1)
+    for side, slot in enumerate((right * 2 + other, left * 2 + other)):
+        push(8, terms.at[slot, lower(0)], rd.at[side], side, to_other)
     for step in range(1, PARTS):
         there = wrap(mine + step, PARTS)
         remote(
@@ -469,8 +474,8 @@
         push(3, terms.at[slot, upper(i)], rb.at[0, i], i, to_right)
         push(4, terms.at[slot, lower(i)], rb.at[1, i], i, to_left)
 
-    def meet(i):
-        rows = rows_at(i)
+    def meet(i, detour=False):
+        rows = upper(i) if detour else rows_at(i)
         wait_bytes(ra.at[1, rows], rs_sem.at[1, i])
         wait_bytes(ra.at[2, rows], rs_sem.at[2, i])
         slot = x * 2 + other
@@ -480,23 +485,33 @@
             + ra[2, rows, :].astype(F32)
         )
         terms[slot, rows, :] = total.astype(BF16)
-        push(7, terms.at[slot, rows], rc.at[2, rows], i, to_other)
-
-    def pass_on(i):
+        push(7, terms.at[slot, rows_at(i)], rc.at[2, rows_at(i)], i, to_other)
+
+    def pass_on(i, detour=False):
         rows = rows_at(i)
         wait_bytes(rb.at[0, i], rs_sem.at[3, i])
         slot = right * 2 + yl
         total = terms[slot, upper(i), :].astype(F32) + rb[0, i].astype(F32)
         terms[slot, upper(i), :] = total.astype(BF16)
+        if detour:
+            wait_bytes(rd.at[0], rs_sem.at[8, 0])
+            total = terms[slot, lower(i), :].astype(F32) + rd[0].astype(F32)
+            terms[slot, lower(i), :] = total.astype(BF16)
         push(5, terms.at[slot, rows], rc.at[0, rows], i, to_right)
         wait_bytes(rb.at[1, i], rs_sem.at[4, i])
         slot = left * 2 + yl
         total = terms[slot, lower(i), :].astype(F32) + rb[1, i].astype(F32)
+        if detour:
+            wait_bytes(rd.at[1], rs_sem.at[8, 1])
+            total = total + rd[1].astype(F32)
         terms[slot, lower(i), :] = total.astype(BF16)
         push(6, terms.at[slot, rows], rc.at[1, rows], i, to_left)
 
-    each_chunk(lambda i: (join(i), meet(i)))
-    each_chunk(pass_on)
+    join(0)
+    meet(0, detour=True)
+    each_chunk(lambda i: (join(i), meet(i)), 1)
+    pass_on(0, detour=True)
+    each_chunk(pass_on, 1)
     lax.fori_loop(0, PARTS, second_grad, 0)
     wait_bytes(inner.at[pl.ds(0, PARTS - 1)], inner_sem)
     acc[...] = jnp.zeros_like(acc)
@@ -596,6 +611,7 @@
             pltpu.VMEM((3, ROWS, WIDTH), BF16),
             pltpu.VMEM((2, CHUNKS, HALF, WIDTH), BF16),
             pltpu.VMEM((3, ROWS, WIDTH), BF16),
+            pltpu.VMEM((2, HALF, WIDTH), BF16),
             pltpu.VMEM((PARTS, 8, CHUNK), F32),
             pltpu.VMEM((PARTS, WIDTH, WIDTH), F32),
             dma((8,)),
@@ -604,7 +620,7 @@
             dma((4, 3)),
             dma((9, CHUNKS)),
             dma((9, CHUNKS)),
-            dma((8, CHUNKS)),
+            dma((9, CHUNKS)),
             dma(()),
         ],
         compiler_params=pltpu.CompilerParams(

time: 145 us -> 144 us (level)
  Pallas kernels: 145 us -> 143 us
where the time goes in v4:
time: 144 us
  Pallas kernels  143 us (99%)
    pallas_call x1, Pallas kernels, shards(): pl.pallas_call(kernel, out_shape=(pltpu.VMEM(anchor.shape, F32), pltpu.VM...  141 us

profile of v4, /device:TPU:1, one launch (start us, length us, event | category | flops | bytes accessed | tf_op | source)
XLA Modules:
  0.0 144.1 jit_solution(18236247580811089046)
XLA Ops:
  0.6 141.4 %shard_map.94 = (f32[16,64,256]{2,1,0:T(8,128)S(1)}, f32[16,64,256]{2,1,0:T(8,128)S(1)}, bf16[1,2,2048,256]{3,2,1,0:T(8,128)(2,1)S(1)}) custom-call(s32[2,32]{1,0:T(2,128)} %bitcast.2, s32[2,32]{1,0:T(2,128)} %bitcast.3, f32[16,64,256]{2,1,0:T(8,128)} %anchor_ref.1, f32[16,64,256]{2,1,0:T(8,128)} %momentum_ref.1, f32[1,2,2048,256]{3,2,1,0:T(8,128)} %deltas_ref.1, ...), custom_call_target="tpu_custom_call" | custom-call | tf_op jit(solution)/shard_map/pallas_call | solution.py:584
  142.1 2.0 %shard_map.95 = (f32[16,64,256]{2,1,0:T(8,128)}, f32[16,64,256]{2,1,0:T(8,128)}, bf16[1,2,2048,256]{3,2,1,0:T(8,128)(2,1)}) custom-call(f32[16,64,256]{2,1,0:T(8,128)S(1)} %get-tuple-element.6.anchor, f32[16,64,256]{2,1,0:T(8,128)S(1)} %get-tuple-element.7.momentum, bf16[1,2,2048,256]{3,2,1,0:T(8,128)(2,1)S(1)} %get-tuple-element.8.grads), custom_call_target="tpu_custom_call" | custom-call | tf_op jit(solution)/shard_map/pallas_call | solution.py:630
